TPU v7x, 32 devices: a whole 2x2x4 slice. The times are simulated.
32 devices in a mesh: groups: 2 (over x), ctx: 16 (over z, y, core).
Axes of the slice: x: 2, y: 2, z: 4, core: 2. Of those that a mesh axis runs over, the one named last changes fastest.
Arguments:
- queries: bfloat16 [512, 128, 576], P(('groups', 'ctx')), parts along dimension 0, may hold values from -4 to 4
- latent_cache: bfloat16 [32768, 576], P(('groups', 'ctx')), parts along dimension 0, may hold values from -4 to 4
- block_picks: int32 [32, 32], P(('groups', 'ctx')), parts along dimension 0, may hold values from 0 to 255, as said below
- lengths: int32 [512], P(('groups', 'ctx')), parts along dimension 0, may hold values from 8192 to 16384
Outputs:
- latent_out: bfloat16 [512, 128, 512], P(('groups', 'ctx')), parts along dimension 0
There are 2 independent parts, one for each index of `groups`. A program takes and returns all parts, laid end to end along the dimension named above; each array names one. Nothing has to cross between parts.
Inputs may be any that keep to these rules, and one draw needn't show every extreme that they name: `block_picks`: each row names 32 different blocks. At most 4 of a row's blocks lie in one owner's range of 16 consecutive blocks, and every row reaches this with its first 4 entries, which lie in the first half of the context. Over all rows together at most 8 different blocks of one owner's range are named, and some owner reaches this.
All inputs are finite; a program needn't handle non-finite values.
Results may differ from a plain program's by a relative error of at most 0.0035.
Values may be sent and summed in bfloat16 or wider, within the bound.
No kernel may reach another device: no remote copies, remote signals or barrier semaphores. Data moves between devices by JAX's collectives and lax.ppermute only.
A program may use at most 128 MiB of HBM per device.

v0:
```python
import jax
import jax.numpy as jnp
from jax import lax
from jax.sharding import PartitionSpec as P

LAT = 512
BLOCK = 64
TOPK = 32
SOFTMAX_SCALE = 192.0 ** (-0.5)


def attend(query_rows, key_rows, positions, row_lengths):
    total_rows = query_rows.shape[0]
    step_rows = 512
    block_count = total_rows // step_rows
    latent = key_rows[:, :LAT]

    def per_block(inputs):
        block_queries, block_lengths = inputs
        block_ratings = (
            lax.dot_general(
                block_queries,
                key_rows,
                (((1,), (1,)), ((), ())),
                preferred_element_type=jnp.float32,
            )
            * SOFTMAX_SCALE
        )
        visible = positions[None, :] < block_lengths[:, None]
        row_max = jnp.max(jnp.where(visible, block_ratings, -jnp.inf), axis=1, keepdims=True)
        exponent = jnp.where(visible, jnp.exp(block_ratings - row_max), 0.0)
        normaliser = jnp.sum(exponent, axis=1, keepdims=True)
        weights = exponent.astype(jnp.bfloat16)
        result = jnp.dot(weights, latent, preferred_element_type=jnp.float32) / normaliser
        return result.astype(jnp.bfloat16)

    outputs = lax.map(
        per_block,
        (
            query_rows.reshape(block_count, step_rows, query_rows.shape[1]),
            row_lengths.reshape(block_count, step_rows),
        ),
    )
    return outputs.reshape(total_rows, LAT)


def shards(queries, latent_cache, block_picks, lengths):
    ctx_count = lax.axis_size("ctx")
    myself = lax.axis_index("ctx")
    feature = latent_cache.shape[1]
    owned = latent_cache.shape[0] // BLOCK
    capacity = max(1, 2 * TOPK // ctx_count)
    block_rows = latent_cache.reshape(owned, BLOCK * feature)
    own_picks = block_picks[0]
    owners = own_picks // owned
    union_size = 2 * capacity
    all_picks = lax.all_gather(block_picks, "ctx", axis=0, tiled=True)
    selected_flag = (
        jnp.zeros((ctx_count * owned,), jnp.int32)
        .at[all_picks.reshape(-1)]
        .set(1)
        .reshape(ctx_count, owned)
    )
    packed_at = jnp.cumsum(selected_flag, axis=1) - 1
    own_flag = lax.dynamic_index_in_dim(selected_flag, myself, 0, keepdims=False)
    own_packed = lax.dynamic_index_in_dim(packed_at, myself, 0, keepdims=False)
    slot_ids = jnp.arange(union_size, dtype=jnp.int32)
    matches = (own_packed[None, :] == slot_ids[:, None]) & (own_flag[None, :] == 1)
    source = jnp.sum(
        matches.astype(jnp.int32) * jnp.arange(owned, dtype=jnp.int32)[None, :], axis=1
    )
    candidates = jnp.take(block_rows, source, axis=0)
    target = owners * union_size + jnp.take(packed_at.reshape(-1), own_picks)
    portion = lax.all_gather(candidates, "ctx", axis=0, tiled=True)
    indices = jnp.arange(portion.shape[0], dtype=jnp.int32)
    pick_one = (target[:, None] == indices[None, :]).astype(jnp.bfloat16)
    chosen = jnp.dot(pick_one, portion, preferred_element_type=jnp.float32).astype(jnp.bfloat16)
    key_rows = chosen.reshape(TOPK * BLOCK, feature)
    within = jnp.arange(BLOCK, dtype=jnp.int32)
    positions = (own_picks[:, None] * BLOCK + within[None, :]).reshape(-1)
    head_count = queries.shape[1]
    query_rows = queries.reshape(queries.shape[0] * head_count, feature)
    row_lengths = jnp.repeat(lengths, head_count)
    result = attend(query_rows, key_rows, positions, row_lengths)
    return result.reshape(queries.shape[0], head_count, LAT)


def solution(mesh):
    placed = (
        P(("groups", "ctx"), None, None),
        P(("groups", "ctx"), None),
        P(("groups", "ctx"), None),
        P(("groups", "ctx")),
    )
    return jax.shard_map(
        shards,
        mesh=mesh,
        in_specs=placed,
        out_specs=P(("groups", "ctx"), None, None),
        check_vma=False,
    )
```

profile of v0, /device:TPU:0, one launch (start us, length us, event | category | flops | bytes accessed | tf_op | source)
XLA Modules:
  0.0 166.6 jit_solution(2164973816998494499)
XLA Ops:
  6.5 23.3 %all-gather = s32[16,1,32]{2,1,0:T(1,128)S(1)} all-gather(s32[1,1,32]{2,1,0:T(1,128)} %bitcast.62), channel_id=1, replica_groups=mesh['groups'=2,'ctx'=16] {'ctx'}, dimensions={0}, use_global_device_ids=true | all-gather | bytes 2176 | tf_op jit(solution)/shard_map/all_gather | solution.py:57
  29.8 0.5 broadcast.185
  30.3 0.7 reduce.3
  31.0 0.1 reshape.149
  31.1 2.4 %scatter_custom_fusion = s32[256]{0:T(256)S(1)} fusion(s32[512]{0:T(512)S(1)} %bitcast.61, s32[512]{0:T(512)S(1)} %broadcast.154, s32[]{:T(128)} %copy.24), kind=kCustom, calls=%fused_computation.56 | custom fusion | bytes 1028 | tf_op jit(solution)/shard_map/scatter | solution.py:61
  33.6 0.2 reduce_window_sum.11
  33.8 0.1 select_reduce_fusion
  34.0 1.7 %copy.12 = bf16[1024,576]{1,0:T(8,128)(2,1)S(1)} copy(bf16[1024,576]{0,1:T(8,128)(2,1)} %param.7) | data formatting | bytes 2359296 | tf_op args[1]
  35.7 1.6 reshape.151
  37.3 1.8 %gather_fusion.1 = bf16[8,36864]{1,0:T(8,128)(2,1)} fusion(bf16[16,36864]{1,0:T(8,128)(2,1)S(1)} %reshape.151, s32[1024]{0:T(1024)S(1)} %pad_clamp_fusion), kind=kCustom, calls=%fused_computation.1 | custom fusion | bytes 1179680 | tf_op jit(solution)/shard_map/jit(_take)/gather | solution.py:72
  39.1 2.0 %broadcast_select_fusion = bf16[8,36864]{1,0:T(8,128)(2,1)} fusion(bf16[8,36864]{1,0:T(8,128)(2,1)} %gather_fusion.1, pred[8]{0:T(512)(128)(4,1)S(1)} %compare_and_fusion), kind=kLoop, calls=%fused_computation.27 | loop fusion | flops 294912 | bytes 1179656 | tf_op jit(solution)/shard_map/jit(_take)/select_n | solution.py:72
  41.1 0.1 sub.22
  41.2 2.6 %copy.11 = bf16[16,128,576]{2,1,0:T(8,128)(2,1)} copy(bf16[16,128,576]{1,2,0:T(8,128)(2,1)S(1)} %copy-done) | data formatting | bytes 4718592 | tf_op args[0]
  43.8 0.1 broadcast_in_dim.55
  43.9 0.7 gather_fusion
  44.7 74.8 %all-gather.3.cloned.1.call-done = bf16[128,36864]{1,0:T(8,128)(2,1)} async-done(((bf16[8,36864]{1,0:T(8,128)(2,1)}), bf16[128,36864]{1,0:T(8,128)(2,1)}) %all-gather.3.cloned.1.call-update) | async-done | bytes 9437200 | tf_op jit(solution)/shard_map/all_gather | solution.py:74
  119.4 5.1 %convolution_convert_fusion = bf16[32,36864]{1,0:T(8,128)(2,1)S(1)} fusion(bf16[128,36864]{1,0:T(8,128)(2,1)} %all-gather.3.cloned.1.call-done, s32[32]{0:T(128)S(1)} %get-tuple-element.77), kind=kOutput, calls=%fused_computation.26 | convolution fusion | flops 303173632 | bytes 11796608 | tf_op jit(solution)/shard_map/dot_general | solution.py:77
  124.5 4.1 %reshape.152 = bf16[2048,576]{1,0:T(8,128)(2,1)} reshape(bf16[32,36864]{1,0:T(8,128)(2,1)S(1)} %convolution_convert_fusion) | data formatting | bytes 4718592 | tf_op jit(solution)/shard_map/reshape | solution.py:78
  128.6 1.6 slice-done
  130.2 29.5 %while.11 = (s32[]{:T(128)}, bf16[4,512,512]{2,1,0:T(8,128)(2,1)}, s32[4,512]{1,0:T(4,128)S(1)}, bf16[4,512,576]{2,1,0:T(8,128)(2,1)}, bf16[2048,576]{1,0:T(8,12...) while((s32[]{:T(128)}, bf16[4,512,512]{2,1,0:T(8,128)(2,1)}, ...), condition=%wide.region_6.7_spmd.clone, body=%wide.region_3.6_spmd.clone.sunk | while | flops 2296906752 | bytes 18552024 | solution.py:37
  130.4 3.9 %fusion.45 = (f32[512]{0:T(512)S(1)}, f32[512,2048]{1,0:T(8,128)S(1)}) fusion(s32[2048]{0:T(1024)S(1)} %lt.139, s32[512]{0:T(512)S(1)} %bitcast.57, bf16[2048,576]{1,0:T(8,128)(2,1)} %get-tuple-element.145, bf16[4,512,576]{2,1,0:T(8,128)(2,1)} %get-tuple-element.144, s32[]{:T(128)} %get-tuple-element.133), kind=kOutput, calls=%fused_computation.6.clone.1 | convolution fusion | flops 1212153344 | bytes 7483904 | tf_op jit(solution)/shard_map/while/body/eval_jaxpr/dot_general | solution.py:21
  134.3 1.1 fusion.46
  135.4 2.2 %fusion.47 = bf16[4,512,512]{2,1,0:T(8,128)(2,1)} fusion(bf16[4,512,512]{2,1,0:T(8,128)(2,1)} %get-tuple-element.134, s32[]{:T(128)} %get-tuple-element.133, bf16[2048,512]{1,0:T(8,128)(2,1)S(1)} %get-tuple-element.146, f32[512,2048]{1,0:T(8,128)S(1)} %get-tuple-element.123, f32[512]{0:T(512)S(1)} %get-tuple-element.124, s32[2048]{0:T(1024)S(1)} %lt.139, ...), kind=kOutput, calls=%fused_computation.17.clone.1 | convolution fusion | flops 1079508992 | bytes 6830592 | tf_op jit(solution)/shard_map/while/body/eval_jaxpr/dot_general | solution.py:34
  137.8 3.9 %fusion.45 = (f32[512]{0:T(512)S(1)}, f32[512,2048]{1,0:T(8,128)S(1)}) fusion(s32[2048]{0:T(1024)S(1)} %lt.139, s32[512]{0:T(512)S(1)} %bitcast.57, bf16[2048,576]{1,0:T(8,128)(2,1)} %get-tuple-element.145, bf16[4,512,576]{2,1,0:T(8,128)(2,1)} %get-tuple-element.144, s32[]{:T(128)} %get-tuple-element.133), kind=kOutput, calls=%fused_computation.6.clone.1 | convolution fusion | flops 1212153344 | bytes 7483904 | tf_op jit(solution)/shard_map/while/body/eval_jaxpr/dot_general | solution.py:21
  141.7 1.1 fusion.46
  142.8 2.2 %fusion.47 = bf16[4,512,512]{2,1,0:T(8,128)(2,1)} fusion(bf16[4,512,512]{2,1,0:T(8,128)(2,1)} %get-tuple-element.134, s32[]{:T(128)} %get-tuple-element.133, bf16[2048,512]{1,0:T(8,128)(2,1)S(1)} %get-tuple-element.146, f32[512,2048]{1,0:T(8,128)S(1)} %get-tuple-element.123, f32[512]{0:T(512)S(1)} %get-tuple-element.124, s32[2048]{0:T(1024)S(1)} %lt.139, ...), kind=kOutput, calls=%fused_computation.17.clone.1 | convolution fusion | flops 1079508992 | bytes 6830592 | tf_op jit(solution)/shard_map/while/body/eval_jaxpr/dot_general | solution.py:34
  145.1 3.9 %fusion.45 = (f32[512]{0:T(512)S(1)}, f32[512,2048]{1,0:T(8,128)S(1)}) fusion(s32[2048]{0:T(1024)S(1)} %lt.139, s32[512]{0:T(512)S(1)} %bitcast.57, bf16[2048,576]{1,0:T(8,128)(2,1)} %get-tuple-element.145, bf16[4,512,576]{2,1,0:T(8,128)(2,1)} %get-tuple-element.144, s32[]{:T(128)} %get-tuple-element.133), kind=kOutput, calls=%fused_computation.6.clone.1 | convolution fusion | flops 1212153344 | bytes 7483904 | tf_op jit(solution)/shard_map/while/body/eval_jaxpr/dot_general | solution.py:21
  149.1 1.1 fusion.46
  150.2 2.2 %fusion.47 = bf16[4,512,512]{2,1,0:T(8,128)(2,1)} fusion(bf16[4,512,512]{2,1,0:T(8,128)(2,1)} %get-tuple-element.134, s32[]{:T(128)} %get-tuple-element.133, bf16[2048,512]{1,0:T(8,128)(2,1)S(1)} %get-tuple-element.146, f32[512,2048]{1,0:T(8,128)S(1)} %get-tuple-element.123, f32[512]{0:T(512)S(1)} %get-tuple-element.124, s32[2048]{0:T(1024)S(1)} %lt.139, ...), kind=kOutput, calls=%fused_computation.17.clone.1 | convolution fusion | flops 1079508992 | bytes 6830592 | tf_op jit(solution)/shard_map/while/body/eval_jaxpr/dot_general | solution.py:34
  152.5 3.9 %fusion.45 = (f32[512]{0:T(512)S(1)}, f32[512,2048]{1,0:T(8,128)S(1)}) fusion(s32[2048]{0:T(1024)S(1)} %lt.139, s32[512]{0:T(512)S(1)} %bitcast.57, bf16[2048,576]{1,0:T(8,128)(2,1)} %get-tuple-element.145, bf16[4,512,576]{2,1,0:T(8,128)(2,1)} %get-tuple-element.144, s32[]{:T(128)} %get-tuple-element.133), kind=kOutput, calls=%fused_computation.6.clone.1 | convolution fusion | flops 1212153344 | bytes 7483904 | tf_op jit(solution)/shard_map/while/body/eval_jaxpr/dot_general | solution.py:21
  156.4 1.1 fusion.46
  157.6 2.2 %fusion.47 = bf16[4,512,512]{2,1,0:T(8,128)(2,1)} fusion(bf16[4,512,512]{2,1,0:T(8,128)(2,1)} %get-tuple-element.134, s32[]{:T(128)} %get-tuple-element.133, bf16[2048,512]{1,0:T(8,128)(2,1)S(1)} %get-tuple-element.146, f32[512,2048]{1,0:T(8,128)S(1)} %get-tuple-element.123, f32[512]{0:T(512)S(1)} %get-tuple-element.124, s32[2048]{0:T(1024)S(1)} %lt.139, ...), kind=kOutput, calls=%fused_computation.17.clone.1 | convolution fusion | flops 1079508992 | bytes 6830592 | tf_op jit(solution)/shard_map/while/body/eval_jaxpr/dot_general | solution.py:34
  (36 shorter events, 0.9 us)
Async XLA Ops:
  6.5 112.9 %all-gather.3.cloned.1.call-start = ((), (), s32[]{:S(2)}) async-start(), calls=%async_computation | async-start | bytes 10027008 | tf_op jit(solution)/shard_map/all_gather | solution.py:74
  37.3 3.9 %copy-start = (bf16[16,128,576]{1,2,0:T(8,128)(2,1)S(1)}, bf16[16,128,576]{1,2,0:T(8,128)(2,1)}, u32[]{:S(2)}) copy-start(bf16[16,128,576]{1,2,0:T(8,128)(2,1)} %param.6) | copy-start | bytes 7077892
  39.1 4.7 %copy-start.2 = (s32[16]{0:T(128)S(1)}, s32[16]{0:T(128)}, u32[]{:S(2)}) copy-start(s32[16]{0:T(128)} %param.9) | copy-start | bytes 196
  39.1 4.9 %copy-start.1 = (s32[1,32]{1,0:T(1,128)S(1)}, s32[1,32]{1,0:T(1,128)}, u32[]{:S(2)}) copy-start(s32[1,32]{1,0:T(1,128)} %param.8) | copy-start | bytes 388
  128.6 1.6 slice-start
Sparse Core Ops, SparseCore 0:
  41.2 78.1 all-gather.2
where the time goes:
time: 167 us
  waiting for transfers between devices  74.8 us (45%)
  matrix products  29.5 us (18%)
  blocking collectives  23.3 us (14%)
  local copies, waits for them, and re-layouts  17.7 us (11%)
  between operations  13.5 us (8%)
  other arithmetic  7.79 us (5%)
    all_gather x1, waiting for transfers between devices, shards(): portion = lax.all_gather(candidates, 'ctx', axis=0, tiled=True)  74.8 us
    all_gather x1, blocking collectives, shards(): all_picks = lax.all_gather(block_picks, 'ctx', axis=0, tiled=True)  23.3 us
    dot_general x4, matrix products, per_block(): lax.dot_general(block_queries, key_rows, (((1,), (1,)), ((), ())), prefer...  15.7 us
    dot_general x4, matrix products, per_block(): jnp.dot(weights, latent, preferred_element_type=jnp.float32) / normaliser  8.69 us
    dot_general x1, matrix products, shards(): jnp.dot(pick_one, portion, preferred_element_type=jnp.float32)  5.07 us
    reduce_sum x4, other arithmetic, per_block(): normaliser = jnp.sum(exponent, axis=1, keepdims=True)  4.46 us
    unnamed x10, local copies, waits for them, and re-layouts  4.33 us
    reshape x1, local copies, waits for them, and re-layouts, shards(): key_rows = chosen.reshape(TOPK * BLOCK, feature)  4.14 us
  transfers between devices with their start and end apart: 1, of which 1 were waited for; matrix products, arithmetic and copies ran while one was open for 2% of the time, Pallas kernels for 0%

commit v1 on v0

--- a/solution.py
+++ b/solution.py
@@ -54,7 +54,12 @@
     own_picks = block_picks[0]
     owners = own_picks // owned
     union_size = 2 * capacity
-    all_picks = lax.all_gather(block_picks, "ctx", axis=0, tiled=True)
+    ring = [block_picks]
+    for hop in range(15):
+        ring.append(lax.ppermute(ring[-1], "ctx", [(dev, (dev + 1) % 16) for dev in range(16)]))
+    all_picks = jnp.roll(
+        jnp.concatenate(ring[::-1], axis=0), (lax.axis_index("ctx") + 1) * ring[0].shape[0], axis=0
+    )
     selected_flag = (
         jnp.zeros((ctx_count * owned,), jnp.int32)
         .at[all_picks.reshape(-1)]

time: 167 us -> 233 us (1.40)
  waiting for transfers between devices: 74.8 us -> 157 us
  blocking collectives: 23.3 us -> 0 us
  local copies, waits for them, and re-layouts: 17.7 us -> 23.8 us
    ppermute x0 -> x15, waiting for transfers between devices: none -> 82 us  [shards(): lax.ppermute(ring[-1], 'ctx', [(dev, (dev + 1) % 16) for dev in range(16)])]
    all_gather x1 -> x0, blocking collectives: 23.3 us -> none  [shards(): all_picks = lax.all_gather(block_picks, 'ctx', axis=0, tiled=True)]
    concatenate x0 -> x1, local copies, waits for them, and re-layouts: none -> 2.89 us  [shards(): jnp.roll(jnp.concatenate(ring[::-1], axis=0), (lax.axis_index('ctx') + 1)...]
    unnamed x10 -> x38, local copies, waits for them, and re-layouts: 4.33 us -> 5.46 us
  transfers between devices with their start and end apart: 1 -> 16, of which waited for: 1 -> 16; matrix products, arithmetic and copies ran while one was open for 2% -> 3% of each run, Pallas kernels for 0% -> 0%
where the time goes in v1:
time: 233 us
  waiting for transfers between devices  157 us (67%)
  matrix products  29.5 us (13%)
  local copies, waits for them, and re-layouts  23.8 us (10%)
  between operations  13.6 us (6%)
  other arithmetic  8.45 us (4%)
    ppermute x15, waiting for transfers between devices, shards(): lax.ppermute(ring[-1], 'ctx', [(dev, (dev + 1) % 16) for dev in range(16)])  82 us
    all_gather x1, waiting for transfers between devices, shards(): portion = lax.all_gather(candidates, 'ctx', axis=0, tiled=True)  75.2 us
    dot_general x4, matrix products, per_block(): lax.dot_general(block_queries, key_rows, (((1,), (1,)), ((), ())), prefer...  15.7 us
    dot_general x4, matrix products, per_block(): jnp.dot(weights, latent, preferred_element_type=jnp.float32) / normaliser  8.69 us
    unnamed x38, local copies, waits for them, and re-layouts  5.46 us
    dot_general x1, matrix products, shards(): jnp.dot(pick_one, portion, preferred_element_type=jnp.float32)  5.07 us
  transfers between devices with their start and end apart: 16, of which 16 were waited for; matrix products, arithmetic and copies ran while one was open for 3% of the time, Pallas kernels for 0%

profile of v1, /device:TPU:0, one launch (start us, length us, event | category | flops | bytes accessed | tf_op | source)
XLA Modules:
  0.0 233.1 jit_solution(13429192907913369566)
XLA Ops:
  7.0 6.4 %collective-permute-done = s32[1,32]{1,0:T(1,128)S(1)} collective-permute-done((s32[1,32]{1,0:T(1,128)}, s32[1,32]{1,0:T(1,128)S(1)}, u32[]{:S(2)}, u32[]{:S(2)}) %collective-permute-start) | collective-permute-done | bytes 160 | tf_op jit(solution)/shard_map/ppermute | solution.py:59
  14.0 5.7 %collective-permute-done.1 = s32[1,32]{1,0:T(1,128)S(1)} collective-permute-done((s32[1,32]{1,0:T(1,128)S(1)}, s32[1,32]{1,0:T(1,128)S(1)}, u32[]{:S(2)}, u32[]{:S(2)}) %collective-permute-start.1) | collective-permute-done | bytes 160 | tf_op jit(solution)/shard_map/ppermute | solution.py:59
  19.7 5.7 %collective-permute-done.2 = s32[1,32]{1,0:T(1,128)S(1)} collective-permute-done((s32[1,32]{1,0:T(1,128)S(1)}, s32[1,32]{1,0:T(1,128)S(1)}, u32[]{:S(2)}, u32[]{:S(2)}) %collective-permute-start.2) | collective-permute-done | bytes 160 | tf_op jit(solution)/shard_map/ppermute | solution.py:59
  25.4 5.7 %collective-permute-done.3 = s32[1,32]{1,0:T(1,128)S(1)} collective-permute-done((s32[1,32]{1,0:T(1,128)S(1)}, s32[1,32]{1,0:T(1,128)S(1)}, u32[]{:S(2)}, u32[]{:S(2)}) %collective-permute-start.3) | collective-permute-done | bytes 160 | tf_op jit(solution)/shard_map/ppermute | solution.py:59
  31.1 5.7 %collective-permute-done.4 = s32[1,32]{1,0:T(1,128)S(1)} collective-permute-done((s32[1,32]{1,0:T(1,128)S(1)}, s32[1,32]{1,0:T(1,128)S(1)}, u32[]{:S(2)}, u32[]{:S(2)}) %collective-permute-start.4) | collective-permute-done | bytes 160 | tf_op jit(solution)/shard_map/ppermute | solution.py:59
  36.7 5.7 %collective-permute-done.5 = s32[1,32]{1,0:T(1,128)S(1)} collective-permute-done((s32[1,32]{1,0:T(1,128)S(1)}, s32[1,32]{1,0:T(1,128)S(1)}, u32[]{:S(2)}, u32[]{:S(2)}) %collective-permute-start.5) | collective-permute-done | bytes 160 | tf_op jit(solution)/shard_map/ppermute | solution.py:59
  42.4 5.7 %collective-permute-done.6 = s32[1,32]{1,0:T(1,128)S(1)} collective-permute-done((s32[1,32]{1,0:T(1,128)S(1)}, s32[1,32]{1,0:T(1,128)S(1)}, u32[]{:S(2)}, u32[]{:S(2)}) %collective-permute-start.6) | collective-permute-done | bytes 160 | tf_op jit(solution)/shard_map/ppermute | solution.py:59
  48.1 5.7 %collective-permute-done.7 = s32[1,32]{1,0:T(1,128)S(1)} collective-permute-done((s32[1,32]{1,0:T(1,128)S(1)}, s32[1,32]{1,0:T(1,128)S(1)}, u32[]{:S(2)}, u32[]{:S(2)}) %collective-permute-start.7) | collective-permute-done | bytes 160 | tf_op jit(solution)/shard_map/ppermute | solution.py:59
  53.8 5.7 %collective-permute-done.8 = s32[1,32]{1,0:T(1,128)S(1)} collective-permute-done((s32[1,32]{1,0:T(1,128)S(1)}, s32[1,32]{1,0:T(1,128)S(1)}, u32[]{:S(2)}, u32[]{:S(2)}) %collective-permute-start.8) | collective-permute-done | bytes 160 | tf_op jit(solution)/shard_map/ppermute | solution.py:59
  59.5 5.7 %collective-permute-done.9 = s32[1,32]{1,0:T(1,128)S(1)} collective-permute-done((s32[1,32]{1,0:T(1,128)S(1)}, s32[1,32]{1,0:T(1,128)S(1)}, u32[]{:S(2)}, u32[]{:S(2)}) %collective-permute-start.9) | collective-permute-done | bytes 160 | tf_op jit(solution)/shard_map/ppermute | solution.py:59
  65.2 5.7 %collective-permute-done.10 = s32[1,32]{1,0:T(1,128)S(1)} collective-permute-done((s32[1,32]{1,0:T(1,128)S(1)}, s32[1,32]{1,0:T(1,128)S(1)}, u32[]{:S(2)}, u32[]{:S(2)}) %collective-permute-start.10) | collective-permute-done | bytes 160 | tf_op jit(solution)/shard_map/ppermute | solution.py:59
  70.9 5.7 %collective-permute-done.11 = s32[1,32]{1,0:T(1,128)S(1)} collective-permute-done((s32[1,32]{1,0:T(1,128)S(1)}, s32[1,32]{1,0:T(1,128)S(1)}, u32[]{:S(2)}, u32[]{:S(2)}) %collective-permute-start.11) | collective-permute-done | bytes 160 | tf_op jit(solution)/shard_map/ppermute | solution.py:59
  76.6 5.7 %collective-permute-done.12 = s32[1,32]{1,0:T(1,128)S(1)} collective-permute-done((s32[1,32]{1,0:T(1,128)S(1)}, s32[1,32]{1,0:T(1,128)S(1)}, u32[]{:S(2)}, u32[]{:S(2)}) %collective-permute-start.12) | collective-permute-done | bytes 160 | tf_op jit(solution)/shard_map/ppermute | solution.py:59
  85.7 2.3 collective-permute-done.13
  88.5 5.1 %collective-permute-done.14 = s32[1,32]{1,0:T(1,128)} collective-permute-done((s32[1,32]{1,0:T(1,128)S(1)}, s32[1,32]{1,0:T(1,128)}, u32[]{:S(2)}, u32[]{:S(2)}) %collective-permute-start.14) | collective-permute-done | bytes 160 | tf_op jit(solution)/shard_map/ppermute | solution.py:59
  93.6 2.9 %concatenate.6 = s32[32,32]{1,0:T(8,128)S(1)} concatenate(s32[1,32]{1,0:T(1,128)} %collective-permute-done.14, s32[1,32]{1,0:T(1,128)} %copy-done.15, s32[1,32]{1,0:T(1,128)} %copy-done.14, s32[1,32]{1,0:T(1,128)} %copy-done.13, s32[1,32]{1,0:T(1,128)} %copy-done.12, s32[1,32]{1,0:T(1,128)} %copy-done.11, s32[1,32]{1,0:T(1,128)} %copy-done.10, s32[1,32]{1,0:T(1,128)} %copy-done.9, ...), dimensions={0} | concatenate | bytes 8192 | tf_op jit(solution)/shard_map/jit(_roll_dynamic)/concatenate | solution.py:60
  97.9 3.0 %scatter_custom_fusion = s32[256]{0:T(256)} fusion(s32[512]{0:T(512)S(1)} %bitcast.60, s32[512]{0:T(512)S(1)} %broadcast.155, s32[]{:T(128)} %copy.22), kind=kCustom, calls=%fused_computation.59 | custom fusion | bytes 1028 | tf_op jit(solution)/shard_map/scatter | solution.py:66
  103.3 1.8 gather_fusion.1
  105.1 2.1 broadcast_select_fusion
  107.2 2.6 %copy.9 = bf16[16,128,576]{2,1,0:T(8,128)(2,1)} copy(bf16[16,128,576]{1,2,0:T(8,128)(2,1)S(1)} %copy-done) | data formatting | bytes 4718592 | tf_op args[0]
  110.7 75.2 %all-gather.2.cloned.1.call-done = bf16[128,36864]{1,0:T(8,128)(2,1)} async-done(((bf16[8,36864]{1,0:T(8,128)(2,1)}), bf16[128,36864]{1,0:T(8,128)(2,1)}) %all-gather.2.cloned.1.call-update) | async-done | bytes 9437200 | tf_op jit(solution)/shard_map/all_gather | solution.py:79
  185.9 5.1 %convolution_convert_fusion = bf16[32,36864]{1,0:T(8,128)(2,1)S(1)} fusion(bf16[128,36864]{1,0:T(8,128)(2,1)} %all-gather.2.cloned.1.call-done, s32[32]{0:T(128)S(1)} %get-tuple-element.77), kind=kOutput, calls=%fused_computation.26 | convolution fusion | flops 303173632 | bytes 11796608 | tf_op jit(solution)/shard_map/dot_general | solution.py:82
  191.0 4.2 %reshape.152 = bf16[2048,576]{1,0:T(8,128)(2,1)} reshape(bf16[32,36864]{1,0:T(8,128)(2,1)S(1)} %convolution_convert_fusion) | data formatting | bytes 4718592 | tf_op jit(solution)/shard_map/reshape | solution.py:83
  196.7 29.5 %while.11 = (s32[]{:T(128)}, bf16[4,512,512]{2,1,0:T(8,128)(2,1)}, s32[4,512]{1,0:T(4,128)S(1)}, bf16[4,512,576]{2,1,0:T(8,128)(2,1)}, bf16[2048,576]{1,0:T(8,12...) while((s32[]{:T(128)}, bf16[4,512,512]{2,1,0:T(8,128)(2,1)}, ...), condition=%wide.region_6.7_spmd.clone, body=%wide.region_3.6_spmd.clone.sunk | while | flops 2296906752 | bytes 18552024 | solution.py:37
  196.9 3.9 %fusion.46 = (f32[512]{0:T(512)S(1)}, f32[512,2048]{1,0:T(8,128)S(1)}) fusion(s32[2048]{0:T(1024)S(1)} %lt.153, s32[512]{0:T(512)S(1)} %bitcast.56, bf16[2048,576]{1,0:T(8,128)(2,1)} %get-tuple-element.145, bf16[4,512,576]{2,1,0:T(8,128)(2,1)} %get-tuple-element.144, s32[]{:T(128)} %get-tuple-element.133), kind=kOutput, calls=%fused_computation.6.clone.1 | convolution fusion | flops 1212153344 | bytes 7483904 | tf_op jit(solution)/shard_map/while/body/eval_jaxpr/dot_general | solution.py:21
  201.9 2.2 fusion.48
  204.2 3.9 %fusion.46 = (f32[512]{0:T(512)S(1)}, f32[512,2048]{1,0:T(8,128)S(1)}) fusion(s32[2048]{0:T(1024)S(1)} %lt.153, s32[512]{0:T(512)S(1)} %bitcast.56, bf16[2048,576]{1,0:T(8,128)(2,1)} %get-tuple-element.145, bf16[4,512,576]{2,1,0:T(8,128)(2,1)} %get-tuple-element.144, s32[]{:T(128)} %get-tuple-element.133), kind=kOutput, calls=%fused_computation.6.clone.1 | convolution fusion | flops 1212153344 | bytes 7483904 | tf_op jit(solution)/shard_map/while/body/eval_jaxpr/dot_general | solution.py:21
  209.3 2.2 fusion.48
  211.6 3.9 %fusion.46 = (f32[512]{0:T(512)S(1)}, f32[512,2048]{1,0:T(8,128)S(1)}) fusion(s32[2048]{0:T(1024)S(1)} %lt.153, s32[512]{0:T(512)S(1)} %bitcast.56, bf16[2048,576]{1,0:T(8,128)(2,1)} %get-tuple-element.145, bf16[4,512,576]{2,1,0:T(8,128)(2,1)} %get-tuple-element.144, s32[]{:T(128)} %get-tuple-element.133), kind=kOutput, calls=%fused_computation.6.clone.1 | convolution fusion | flops 1212153344 | bytes 7483904 | tf_op jit(solution)/shard_map/while/body/eval_jaxpr/dot_general | solution.py:21
  216.7 2.2 fusion.48
  219.0 3.9 %fusion.46 = (f32[512]{0:T(512)S(1)}, f32[512,2048]{1,0:T(8,128)S(1)}) fusion(s32[2048]{0:T(1024)S(1)} %lt.153, s32[512]{0:T(512)S(1)} %bitcast.56, bf16[2048,576]{1,0:T(8,128)(2,1)} %get-tuple-element.145, bf16[4,512,576]{2,1,0:T(8,128)(2,1)} %get-tuple-element.144, s32[]{:T(128)} %get-tuple-element.133), kind=kOutput, calls=%fused_computation.6.clone.1 | convolution fusion | flops 1212153344 | bytes 7483904 | tf_op jit(solution)/shard_map/while/body/eval_jaxpr/dot_general | solution.py:21
  224.0 2.2 fusion.48
  (93 shorter events, 16.4 us)
Async XLA Ops:
  6.5 179.3 %all-gather.2.cloned.1.call-start = ((), (), s32[]{:S(2)}) async-start(), calls=%async_computation | async-start | bytes 10027008 | tf_op jit(solution)/shard_map/all_gather | solution.py:79
  6.5 6.9 %collective-permute-start = (s32[1,32]{1,0:T(1,128)}, s32[1,32]{1,0:T(1,128)S(1)}, u32[]{:S(2)}, u32[]{:S(2)}) collective-permute-start(s32[1,32]{1,0:T(1,128)} %param.8), channel_id=1, source_target_pairs={{0,1},{1,2},{2,3},{3,4},{4,5},{5,6},{6,7},{7,8},{8,9},{9,10},{10,1... | collective-permute-start | bytes 392 | tf_op jit(solution)/shard_map/ppermute | solution.py:59
  14.0 5.7 %collective-permute-start.1 = (s32[1,32]{1,0:T(1,128)S(1)}, s32[1,32]{1,0:T(1,128)S(1)}, u32[]{:S(2)}, u32[]{:S(2)}) collective-permute-start(s32[1,32]{1,0:T(1,128)S(1)} %collective-permute-done), channel_id=1, source_target_pairs={{0,1},{1,2},{2,3},{3,4},{4,5},{5,6},{6,7},{7,8},{8,9},{9,10},{10,1... | collective-permute-start | bytes 392 | tf_op jit(solution)/shard_map/ppermute | solution.py:59
  19.7 62.6 %copy-start.3 = (s32[1,32]{1,0:T(1,128)}, s32[1,32]{1,0:T(1,128)S(1)}, u32[]{:S(2)}) copy-start(s32[1,32]{1,0:T(1,128)S(1)} %collective-permute-done.1) | copy-start | bytes 388
  19.7 5.7 %collective-permute-start.2 = (s32[1,32]{1,0:T(1,128)S(1)}, s32[1,32]{1,0:T(1,128)S(1)}, u32[]{:S(2)}, u32[]{:S(2)}) collective-permute-start(s32[1,32]{1,0:T(1,128)S(1)} %collective-permute-done.1), channel_id=1, source_target_pairs={{0,1},{1,2},{2,3},{3,4},{4,5},{5,6},{6,7},{7,8},{8,9},{9,10},{10,1... | collective-permute-start | bytes 392 | tf_op jit(solution)/shard_map/ppermute | solution.py:59
  25.4 56.9 %copy-start.4 = (s32[1,32]{1,0:T(1,128)}, s32[1,32]{1,0:T(1,128)S(1)}, u32[]{:S(2)}) copy-start(s32[1,32]{1,0:T(1,128)S(1)} %collective-permute-done.2) | copy-start | bytes 388
  25.4 5.7 %collective-permute-start.3 = (s32[1,32]{1,0:T(1,128)S(1)}, s32[1,32]{1,0:T(1,128)S(1)}, u32[]{:S(2)}, u32[]{:S(2)}) collective-permute-start(s32[1,32]{1,0:T(1,128)S(1)} %collective-permute-done.2), channel_id=1, source_target_pairs={{0,1},{1,2},{2,3},{3,4},{4,5},{5,6},{6,7},{7,8},{8,9},{9,10},{10,1... | collective-permute-start | bytes 392 | tf_op jit(solution)/shard_map/ppermute | solution.py:59
  31.0 51.3 %copy-start.5 = (s32[1,32]{1,0:T(1,128)}, s32[1,32]{1,0:T(1,128)S(1)}, u32[]{:S(2)}) copy-start(s32[1,32]{1,0:T(1,128)S(1)} %collective-permute-done.3) | copy-start | bytes 388
  31.1 5.7 %collective-permute-start.4 = (s32[1,32]{1,0:T(1,128)S(1)}, s32[1,32]{1,0:T(1,128)S(1)}, u32[]{:S(2)}, u32[]{:S(2)}) collective-permute-start(s32[1,32]{1,0:T(1,128)S(1)} %collective-permute-done.3), channel_id=1, source_target_pairs={{0,1},{1,2},{2,3},{3,4},{4,5},{5,6},{6,7},{7,8},{8,9},{9,10},{10,1... | collective-permute-start | bytes 392 | tf_op jit(solution)/shard_map/ppermute | solution.py:59
  36.7 45.6 %copy-start.6 = (s32[1,32]{1,0:T(1,128)}, s32[1,32]{1,0:T(1,128)S(1)}, u32[]{:S(2)}) copy-start(s32[1,32]{1,0:T(1,128)S(1)} %collective-permute-done.4) | copy-start | bytes 388
  36.7 5.7 %collective-permute-start.5 = (s32[1,32]{1,0:T(1,128)S(1)}, s32[1,32]{1,0:T(1,128)S(1)}, u32[]{:S(2)}, u32[]{:S(2)}) collective-permute-start(s32[1,32]{1,0:T(1,128)S(1)} %collective-permute-done.4), channel_id=1, source_target_pairs={{0,1},{1,2},{2,3},{3,4},{4,5},{5,6},{6,7},{7,8},{8,9},{9,10},{10,1... | collective-permute-start | bytes 392 | tf_op jit(solution)/shard_map/ppermute | solution.py:59
  42.4 39.9 %copy-start.7 = (s32[1,32]{1,0:T(1,128)}, s32[1,32]{1,0:T(1,128)S(1)}, u32[]{:S(2)}) copy-start(s32[1,32]{1,0:T(1,128)S(1)} %collective-permute-done.5) | copy-start | bytes 388
  42.4 5.7 %collective-permute-start.6 = (s32[1,32]{1,0:T(1,128)S(1)}, s32[1,32]{1,0:T(1,128)S(1)}, u32[]{:S(2)}, u32[]{:S(2)}) collective-permute-start(s32[1,32]{1,0:T(1,128)S(1)} %collective-permute-done.5), channel_id=1, source_target_pairs={{0,1},{1,2},{2,3},{3,4},{4,5},{5,6},{6,7},{7,8},{8,9},{9,10},{10,1... | collective-permute-start | bytes 392 | tf_op jit(solution)/shard_map/ppermute | solution.py:59
  48.1 34.2 %copy-start.8 = (s32[1,32]{1,0:T(1,128)}, s32[1,32]{1,0:T(1,128)S(1)}, u32[]{:S(2)}) copy-start(s32[1,32]{1,0:T(1,128)S(1)} %collective-permute-done.6) | copy-start | bytes 388
  48.1 5.7 %collective-permute-start.7 = (s32[1,32]{1,0:T(1,128)S(1)}, s32[1,32]{1,0:T(1,128)S(1)}, u32[]{:S(2)}, u32[]{:S(2)}) collective-permute-start(s32[1,32]{1,0:T(1,128)S(1)} %collective-permute-done.6), channel_id=1, source_target_pairs={{0,1},{1,2},{2,3},{3,4},{4,5},{5,6},{6,7},{7,8},{8,9},{9,10},{10,1... | collective-permute-start | bytes 392 | tf_op jit(solution)/shard_map/ppermute | solution.py:59
  53.8 28.5 %copy-start.9 = (s32[1,32]{1,0:T(1,128)}, s32[1,32]{1,0:T(1,128)S(1)}, u32[]{:S(2)}) copy-start(s32[1,32]{1,0:T(1,128)S(1)} %collective-permute-done.7) | copy-start | bytes 388
  53.8 5.7 %collective-permute-start.8 = (s32[1,32]{1,0:T(1,128)S(1)}, s32[1,32]{1,0:T(1,128)S(1)}, u32[]{:S(2)}, u32[]{:S(2)}) collective-permute-start(s32[1,32]{1,0:T(1,128)S(1)} %collective-permute-done.7), channel_id=1, source_target_pairs={{0,1},{1,2},{2,3},{3,4},{4,5},{5,6},{6,7},{7,8},{8,9},{9,10},{10,1... | collective-permute-start | bytes 392 | tf_op jit(solution)/shard_map/ppermute | solution.py:59
  59.5 22.8 %copy-start.10 = (s32[1,32]{1,0:T(1,128)}, s32[1,32]{1,0:T(1,128)S(1)}, u32[]{:S(2)}) copy-start(s32[1,32]{1,0:T(1,128)S(1)} %collective-permute-done.8) | copy-start | bytes 388
  59.5 5.7 %collective-permute-start.9 = (s32[1,32]{1,0:T(1,128)S(1)}, s32[1,32]{1,0:T(1,128)S(1)}, u32[]{:S(2)}, u32[]{:S(2)}) collective-permute-start(s32[1,32]{1,0:T(1,128)S(1)} %collective-permute-done.8), channel_id=1, source_target_pairs={{0,1},{1,2},{2,3},{3,4},{4,5},{5,6},{6,7},{7,8},{8,9},{9,10},{10,1... | collective-permute-start | bytes 392 | tf_op jit(solution)/shard_map/ppermute | solution.py:59
  65.2 17.2 %copy-start.11 = (s32[1,32]{1,0:T(1,128)}, s32[1,32]{1,0:T(1,128)S(1)}, u32[]{:S(2)}) copy-start(s32[1,32]{1,0:T(1,128)S(1)} %collective-permute-done.9) | copy-start | bytes 388
  65.2 5.7 %collective-permute-start.10 = (s32[1,32]{1,0:T(1,128)S(1)}, s32[1,32]{1,0:T(1,128)S(1)}, u32[]{:S(2)}, u32[]{:S(2)}) collective-permute-start(s32[1,32]{1,0:T(1,128)S(1)} %collective-permute-done.9), channel_id=1, source_target_pairs={{0,1},{1,2},{2,3},{3,4},{4,5},{5,6},{6,7},{7,8},{8,9},{9,10},{10,1... | collective-permute-start | bytes 392 | tf_op jit(solution)/shard_map/ppermute | solution.py:59
  70.9 11.5 %copy-start.12 = (s32[1,32]{1,0:T(1,128)}, s32[1,32]{1,0:T(1,128)S(1)}, u32[]{:S(2)}) copy-start(s32[1,32]{1,0:T(1,128)S(1)} %collective-permute-done.10) | copy-start | bytes 388
  70.9 5.7 %collective-permute-start.11 = (s32[1,32]{1,0:T(1,128)S(1)}, s32[1,32]{1,0:T(1,128)S(1)}, u32[]{:S(2)}, u32[]{:S(2)}) collective-permute-start(s32[1,32]{1,0:T(1,128)S(1)} %collective-permute-done.10), channel_id=1, source_target_pairs={{0,1},{1,2},{2,3},{3,4},{4,5},{5,6},{6,7},{7,8},{8,9},{9,10},{10,1... | collective-permute-start | bytes 392 | tf_op jit(solution)/shard_map/ppermute | solution.py:59
  76.6 5.8 %copy-start.13 = (s32[1,32]{1,0:T(1,128)}, s32[1,32]{1,0:T(1,128)S(1)}, u32[]{:S(2)}) copy-start(s32[1,32]{1,0:T(1,128)S(1)} %collective-permute-done.11) | copy-start | bytes 388
  76.6 5.7 %collective-permute-start.12 = (s32[1,32]{1,0:T(1,128)S(1)}, s32[1,32]{1,0:T(1,128)S(1)}, u32[]{:S(2)}, u32[]{:S(2)}) collective-permute-start(s32[1,32]{1,0:T(1,128)S(1)} %collective-permute-done.11), channel_id=1, source_target_pairs={{0,1},{1,2},{2,3},{3,4},{4,5},{5,6},{6,7},{7,8},{8,9},{9,10},{10,1... | collective-permute-start | bytes 392 | tf_op jit(solution)/shard_map/ppermute | solution.py:59
  82.3 5.7 %copy-start.14 = (s32[1,32]{1,0:T(1,128)}, s32[1,32]{1,0:T(1,128)S(1)}, u32[]{:S(2)}) copy-start(s32[1,32]{1,0:T(1,128)S(1)} %collective-permute-done.12) | copy-start | bytes 388
  82.3 5.7 %collective-permute-start.13 = (s32[1,32]{1,0:T(1,128)S(1)}, s32[1,32]{1,0:T(1,128)S(1)}, u32[]{:S(2)}, u32[]{:S(2)}) collective-permute-start(s32[1,32]{1,0:T(1,128)S(1)} %collective-permute-done.12), channel_id=1, source_target_pairs={{0,1},{1,2},{2,3},{3,4},{4,5},{5,6},{6,7},{7,8},{8,9},{9,10},{10,1... | collective-permute-start | bytes 392 | tf_op jit(solution)/shard_map/ppermute | solution.py:59
  85.7 21.4 %copy-start = (bf16[16,128,576]{1,2,0:T(8,128)(2,1)S(1)}, bf16[16,128,576]{1,2,0:T(8,128)(2,1)}, u32[]{:S(2)}) copy-start(bf16[16,128,576]{1,2,0:T(8,128)(2,1)} %param.6) | copy-start | bytes 7077892
  88.0 5.6 %collective-permute-start.14 = (s32[1,32]{1,0:T(1,128)S(1)}, s32[1,32]{1,0:T(1,128)}, u32[]{:S(2)}, u32[]{:S(2)}) collective-permute-start(s32[1,32]{1,0:T(1,128)S(1)} %collective-permute-done.13), channel_id=1, source_target_pairs={{0,1},{1,2},{2,3},{3,4},{4,5},{5,6},{6,7},{7,8},{8,9},{9,10},{10,1... | collective-permute-start | bytes 392 | tf_op jit(solution)/shard_map/ppermute | solution.py:59
  105.0 4.7 %copy-start.16 = (s32[16]{0:T(128)S(1)}, s32[16]{0:T(128)}, u32[]{:S(2)}) copy-start(s32[16]{0:T(128)} %param.9) | copy-start | bytes 196
  105.0 4.8 %copy-start.1 = (s32[1,32]{1,0:T(1,128)S(1)}, s32[1,32]{1,0:T(1,128)}, u32[]{:S(2)}) copy-start(s32[1,32]{1,0:T(1,128)} %param.8) | copy-start | bytes 388
  195.1 1.6 slice-start
  (2 other events, 1.1 us)
Sparse Core Ops, SparseCore 0:
  107.3 78.5 all-gather.1
